TPU v7x, 32 devices: a whole 2x2x4 slice. The times are simulated.
32 devices in a mesh: fsdp: 4 (over y, x), tensor: 8 (over z, core).
Axes of the slice: x: 2, y: 2, z: 4, core: 2. Of those that a mesh axis runs over, the one named last changes fastest.
Arguments:
- modality: int32 [4096], P('fsdp'), may hold values from 0 to 2, as said below
- out_grad: bfloat16 [4096, 4096], P('fsdp', 'tensor'), may hold values from -6 to 6
- gate_pre: bfloat16 [4096, 11008], P('fsdp', 'tensor'), may hold values from -6 to 6
- up_pre: bfloat16 [4096, 11008], P('fsdp', 'tensor'), may hold values from -6 to 6
- down_weight: bfloat16 [3, 11008, 4096], P(None, 'tensor', 'fsdp'), may hold values from -0.0546875 to 0.0546875
Outputs:
- down_grad: float32 [3, 11008, 4096], P(None, 'tensor', 'fsdp')
- gate_grad: bfloat16 [4096, 11008], P('fsdp', 'tensor')
- up_grad: bfloat16 [4096, 11008], P('fsdp', 'tensor')
Inputs may be any that keep to these rules, and one draw needn't show every extreme that they name: `modality`: the 1024 tokens of every index of fsdp hold each of the three modalities at least once.
All inputs are finite; a program needn't handle non-finite values.
Results may differ from a plain program's by a relative error of at most 0.012.
Values may be sent and summed in bfloat16 or wider, within the bound.
A program may use at most 256 MiB of HBM per device.

v0:
```python
import jax
import jax.numpy as jnp
from jax import lax
from jax.sharding import PartitionSpec as P


def kind_table(kind_ids):
    labels = jnp.arange(3, dtype=jnp.int32)
    return (kind_ids[:, None] == labels[None, :]).astype(jnp.float32)


def shards(modality, out_grad, gate_pre, up_pre, down_weight):
    tok_rows = modality.shape[0]
    groups = lax.axis_size("fsdp")
    local_onehot = kind_table(modality)
    counts = lax.psum(jnp.sum(local_onehot, axis=0), "fsdp")
    factor = tok_rows * groups / (3.0 * counts)
    token_scale = jnp.sum(local_onehot * factor[None, :], axis=1)
    scaled_part = (out_grad.astype(jnp.float32) * token_scale[:, None]).astype(jnp.bfloat16)
    scaled = lax.all_gather(scaled_part, "tensor", axis=1, tiled=True)
    gate_val = gate_pre.astype(jnp.float32)
    up_val = up_pre.astype(jnp.float32)
    sigmoid_g = jax.nn.sigmoid(gate_val)
    active = gate_val * sigmoid_g
    hidden = (active * up_val).astype(jnp.bfloat16)
    hid_cols = hidden.shape[1]
    kind_marks = local_onehot.T.astype(jnp.bfloat16)
    masked_rows = scaled[None, :, :] * kind_marks[:, :, None]
    folded = lax.dot_general(
        masked_rows,
        lax.all_gather(down_weight, "fsdp", axis=2, tiled=True),
        (((0, 2), (0, 2)), ((), ())),
        preferred_element_type=jnp.float32,
    )
    up_grad = (folded * active).astype(jnp.bfloat16)
    slope = sigmoid_g * (1.0 + gate_val * (1.0 - sigmoid_g))
    gate_grad = (folded * up_val * slope).astype(jnp.bfloat16)
    stacked = jnp.broadcast_to(hidden[None, :, :], (3, tok_rows, hid_cols))
    partial_sum = lax.dot_general(
        stacked, masked_rows, (((1,), (1,)), ((0,), (0,))), preferred_element_type=jnp.float32
    )
    down_grad = lax.psum_scatter(
        partial_sum.astype(jnp.bfloat16), "fsdp", scatter_dimension=2, tiled=True
    ).astype(jnp.float32)
    return (down_grad, gate_grad, up_grad)


def solution(mesh):
    placed = (
        P("fsdp"),
        P("fsdp", "tensor"),
        P("fsdp", "tensor"),
        P("fsdp", "tensor"),
        P(None, "tensor", "fsdp"),
    )
    return jax.shard_map(
        shards,
        mesh=mesh,
        in_specs=placed,
        out_specs=(P(None, "tensor", "fsdp"), P("fsdp", "tensor"), P("fsdp", "tensor")),
        check_vma=False,
    )
```

profile of v0, /device:TPU:0, one launch (start us, length us, event | category | flops | bytes accessed | tf_op | source)
XLA Modules:
  0.0 802.1 jit_solution(10436657843060957811)
XLA Ops:
  7.2 0.0 all-gather.3.cloned.1.call-start
  7.2 0.8 convert_reduce_fusion
  8.0 11.4 %psum.7 = f32[3]{0:T(128)S(1)} all-reduce(f32[3]{0:T(128)S(1)} %convert_reduce_fusion), channel_id=1, replica_groups=mesh['fsdp'=4,'tensor'=8] {'fsdp'}, use_global_device_ids=true, to_apply=%region_1.0 | all-reduce | flops 3 | bytes 24 | tf_op jit(solution)/shard_map/psum | solution.py:16
  19.4 0.8 select_reduce_fusion
  20.2 0.0 copy-start
  20.2 2.5 multiply_convert_fusion
  22.7 0.0 all-gather.3.cloned.1.call-update
  22.7 0.0 all-gather.5.cloned.1.call-start
  22.8 0.7 all-gather.5.cloned.1.call-update
  23.5 0.0 reduce-scatter.2.cloned.1.call-start
  23.5 0.0 copy-done
  23.5 80.7 %all-gather.3.cloned.1.call-done = bf16[1024,4096]{1,0:T(8,128)(2,1)} async-done(((bf16[1024,512]{1,0:T(8,128)(2,1)}), bf16[1024,4096]{1,0:T(8,128)(2,1)}) %all-gather.3.cloned.1.call-update) | async-done | bytes 8388624 | tf_op jit(solution)/shard_map/all_gather | solution.py:20
  104.3 300.9 %all-gather.5.cloned.1.call-done = bf16[3,1376,4096]{2,1,0:T(8,128)(2,1)} async-done(((bf16[3,1376,1024]{2,1,0:T(8,128)(2,1)}), bf16[3,1376,4096]{2,1,0:T(8,128)(2,1)}) %all-gather.5.cloned.1.call-update) | async-done | bytes 33816592 | tf_op jit(solution)/shard_map/all_gather | solution.py:31
  405.2 45.4 %fusion.19 = (bf16[1024,1376]{0,1:T(8,128)(2,1)}, bf16[1024,1376]{0,1:T(8,128)(2,1)}, bf16[1024,1376]{0,1:T(8,128)(2,1)S(1)}) fusion(bf16[1024,1376]{0,1:T(8,128)(2,1)} %param.7, bf16[1024,1376]{0,1:T(8,128)(2,1)} %param.8, bf16[3,1376,4096]{2,1,0:T(8,128)(2,1)} %all-gather.5.cloned.1.call-done, bf16[3,1024]{1,0:T(4,128)(2,1)S(1)} %convert_convert_fusion, ...), kind=kOutput, calls=%fused_computation.23 | convolution fusion | flops 34664710144 | bytes 56301568 | tf_op jit(solution)/shard_map/dot_general | solution.py:29
  450.6 1.1 fusion.28
  451.7 41.3 %fusion.4 = bf16[3,1376,4096]{2,1,0:T(8,128)(2,1)} fusion(bf16[3,1024]{1,0:T(4,128)(2,1)S(1)} %convert_convert_fusion, bf16[1024,4096]{1,0:T(8,128)(2,1)} %all-gather.3.cloned.1.call-done, bf16[3,1024,1376]{1,2,0:T(8,128)(2,1)S(1)} %fusion.28), kind=kOutput, calls=%fused_computation.4 | convolution fusion | flops 34657665024 | bytes 50665472 | tf_op jit(solution)/shard_map/dot_general | solution.py:39
  493.0 0.0 reduce-scatter.2.cloned.1.call-update
  493.0 290.8 %reduce-scatter.2.cloned.1.call-done = bf16[3,1376,1024]{2,1,0:T(8,128)(2,1)} async-done(((bf16[3,1376,4096]{2,1,0:T(8,128)(2,1)}), bf16[3,1376,1024]{2,1,0:T(8,128)(2,1)}) %reduce-scatter.2.cloned.1.call-update) | async-done | bytes 8454160 | tf_op jit(solution)/shard_map/reduce_scatter | solution.py:42
  783.8 11.8 %convert_element_type.53 = f32[3,1376,1024]{2,1,0:T(8,128)} convert(bf16[3,1376,1024]{2,1,0:T(8,128)(2,1)} %reduce-scatter.2.cloned.1.call-done) | non-fusion elementwise | flops 4227072 | bytes 25362432 | tf_op jit(solution)/shard_map/convert_element_type | solution.py:44
  (2 shorter events, 0.0 us)
Async XLA Ops:
  7.2 97.1 %all-gather.3.cloned.1.call-start = ((), (), s32[]{:S(2)}) async-start(), calls=%async_computation.1 | async-start | bytes 9437184 | tf_op jit(solution)/shard_map/all_gather | solution.py:20
  20.2 3.3 copy-start
  22.7 382.5 %all-gather.5.cloned.1.call-start = ((), (), s32[]{:S(2)}) async-start(), calls=%async_computation.3 | async-start | bytes 42270720 | tf_op jit(solution)/shard_map/all_gather | solution.py:31
  23.5 760.4 %reduce-scatter.2.cloned.1.call-start = ((), (), s32[]{:S(2)}) async-start(), calls=%async_computation.2 | async-start | bytes 42270720 | tf_op jit(solution)/shard_map/reduce_scatter | solution.py:42
Sparse Core Ops, SparseCore 0:
  22.8 81.3 all-gather.2
  106.1 298.9 all-gather.4
  493.1 290.6 reduce-scatter.1
where the time goes:
time: 802 us
  waiting for transfers between devices  673 us (84%)
  matrix products  86.7 us (11%)
  other arithmetic  15.9 us (2%)
  between operations  13.8 us (2%)
  blocking collectives  11.4 us (1%)
    all_gather x1, waiting for transfers between devices, shards(): lax.all_gather(down_weight, 'fsdp', axis=2, tiled=True)  301 us
    reduce_scatter x1, waiting for transfers between devices, shards(): lax.psum_scatter(partial_sum.astype(jnp.bfloat16), 'fsdp', scatter_dimens...  291 us
    all_gather x1, waiting for transfers between devices, shards(): scaled = lax.all_gather(scaled_part, 'tensor', axis=1, tiled=True)  80.7 us
    dot_general x1, matrix products, shards(): lax.dot_general(masked_rows, lax.all_gather(down_weight, 'fsdp', axis=2,...  45.4 us
    dot_general x1, matrix products, shards(): lax.dot_general(stacked, masked_rows, (((1,), (1,)), ((0,), (0,))), prefe...  41.3 us
  transfers between devices with their start and end apart: 3, of which 3 were waited for; matrix products, arithmetic and copies ran while one was open for 0% of the time, Pallas kernels for 0%

commit v1 on v0

--- a/solution.py
+++ b/solution.py
@@ -17,7 +17,14 @@
     factor = tok_rows * groups / (3.0 * counts)
     token_scale = jnp.sum(local_onehot * factor[None, :], axis=1)
     scaled_part = (out_grad.astype(jnp.float32) * token_scale[:, None]).astype(jnp.bfloat16)
-    scaled = lax.all_gather(scaled_part, "tensor", axis=1, tiled=True)
+    ring = [scaled_part]
+    for hop in range(7):
+        ring.append(lax.ppermute(ring[-1], "tensor", [(dev, (dev + 1) % 8) for dev in range(8)]))
+    scaled = jnp.roll(
+        jnp.concatenate(ring[::-1], axis=1),
+        (lax.axis_index("tensor") + 1) * ring[0].shape[1],
+        axis=1,
+    )
     gate_val = gate_pre.astype(jnp.float32)
     up_val = up_pre.astype(jnp.float32)
     sigmoid_g = jax.nn.sigmoid(gate_val)

time: 802 us -> 713 us (0.89)
  waiting for transfers between devices: 673 us -> 544 us
  local copies, waits for them, and re-layouts: 1.11 us -> 36.9 us
    all_gather x1, waiting for transfers between devices: 301 us -> 141 us  [shards(): lax.all_gather(down_weight, 'fsdp', axis=2, tiled=True)]
    ppermute x0 -> x7, waiting for transfers between devices: none -> 112 us  [shards(): lax.ppermute(ring[-1], 'tensor', [(dev, (dev + 1) % 8) for dev in range(8)])]
    all_gather x1 -> x0, waiting for transfers between devices: 80.7 us -> none  [shards(): scaled = lax.all_gather(scaled_part, 'tensor', axis=1, tiled=True)]
    unnamed x2 -> x28, local copies, waits for them, and re-layouts: 0.01 us -> 26.4 us
  transfers between devices with their start and end apart: 3 -> 9, of which waited for: 3 -> 9; matrix products, arithmetic and copies ran while one was open for 0% -> 5% of each run, Pallas kernels for 0% -> 0%
where the time goes in v1:
time: 713 us; the launch traced here: 712 us
  waiting for transfers between devices  544 us (76%)
  matrix products  86.9 us (12%)
  local copies, waits for them, and re-layouts  36.9 us (5%)
  other arithmetic  18.8 us (3%)
  between operations  14.1 us (2%)
  blocking collectives  11.4 us (2%)
    reduce_scatter x1, waiting for transfers between devices, shards(): lax.psum_scatter(partial_sum.astype(jnp.bfloat16), 'fsdp', scatter_dimens...  291 us
    all_gather x1, waiting for transfers between devices, shards(): lax.all_gather(down_weight, 'fsdp', axis=2, tiled=True)  141 us
    ppermute x7, waiting for transfers between devices, shards(): lax.ppermute(ring[-1], 'tensor', [(dev, (dev + 1) % 8) for dev in range(8)])  112 us
    dot_general x1, matrix products, shards(): lax.dot_general(masked_rows, lax.all_gather(down_weight, 'fsdp', axis=2,...  45.7 us
    dot_general x1, matrix products, shards(): lax.dot_general(stacked, masked_rows, (((1,), (1,)), ((0,), (0,))), prefe...  41.2 us
    unnamed x28, local copies, waits for them, and re-layouts  26.4 us
  transfers between devices with their start and end apart: 9, of which 9 were waited for; matrix products, arithmetic and copies ran while one was open for 5% of the time, Pallas kernels for 0%

profile of v1, /device:TPU:0, one launch (start us, length us, event | category | flops | bytes accessed | tf_op | source)
XLA Modules:
  0.0 712.4 jit_solution(9087198287868958616)
XLA Ops:
  7.2 0.0 copy-start
  7.2 0.0 all-gather.2.cloned.1.call-start
  7.2 0.7 all-gather.2.cloned.1.call-update
  7.9 0.0 reduce-scatter.2.cloned.1.call-start
  8.0 0.8 convert_reduce_fusion
  8.8 11.4 %psum.7 = f32[3]{0:T(128)S(1)} all-reduce(f32[3]{0:T(128)S(1)} %convert_reduce_fusion), channel_id=1, replica_groups=mesh['fsdp'=4,'tensor'=8] {'fsdp'}, use_global_device_ids=true, to_apply=%region_1.0 | all-reduce | flops 3 | bytes 24 | tf_op jit(solution)/shard_map/psum | solution.py:16
  20.2 0.8 select_reduce_fusion
  20.9 2.1 multiply_convert_fusion
  23.0 0.1 collective-permute-start
  23.1 16.0 %collective-permute-done = bf16[1024,512]{1,0:T(8,128)(2,1)S(1)} collective-permute-done((bf16[1024,512]{1,0:T(8,128)(2,1)S(1)}, bf16[1024,512]{1,0:T(8,128)(2,1)S(1)}, u32[]{:S(2)}, u32[]{:S(2)}) %collective-permute-start) | collective-permute-done | bytes 1048608 | tf_op jit(solution)/shard_map/ppermute | solution.py:22
  39.1 0.0 collective-permute-start.1
  39.1 16.0 %collective-permute-done.1 = bf16[1024,512]{1,0:T(8,128)(2,1)S(1)} collective-permute-done((bf16[1024,512]{1,0:T(8,128)(2,1)S(1)}, bf16[1024,512]{1,0:T(8,128)(2,1)S(1)}, u32[]{:S(2)}, u32[]{:S(2)}) %collective-permute-start.1) | collective-permute-done | bytes 1048608 | tf_op jit(solution)/shard_map/ppermute | solution.py:22
  55.1 0.0 collective-permute-start.2
  55.1 16.0 %collective-permute-done.2 = bf16[1024,512]{1,0:T(8,128)(2,1)S(1)} collective-permute-done((bf16[1024,512]{1,0:T(8,128)(2,1)S(1)}, bf16[1024,512]{1,0:T(8,128)(2,1)S(1)}, u32[]{:S(2)}, u32[]{:S(2)}) %collective-permute-start.2) | collective-permute-done | bytes 1048608 | tf_op jit(solution)/shard_map/ppermute | solution.py:22
  71.1 0.0 copy-start.1
  71.1 1.0 copy-done.1
  72.1 0.0 collective-permute-start.3
  72.1 16.0 %collective-permute-done.3 = bf16[1024,512]{1,0:T(8,128)(2,1)S(1)} collective-permute-done((bf16[1024,512]{1,0:T(8,128)(2,1)S(1)}, bf16[1024,512]{1,0:T(8,128)(2,1)S(1)}, u32[]{:S(2)}, u32[]{:S(2)}) %collective-permute-start.3) | collective-permute-done | bytes 1048608 | tf_op jit(solution)/shard_map/ppermute | solution.py:22
  88.2 0.0 copy-start.3
  88.2 1.0 copy-done.3
  89.1 0.0 collective-permute-start.4
  89.1 16.0 %collective-permute-done.4 = bf16[1024,512]{1,0:T(8,128)(2,1)S(1)} collective-permute-done((bf16[1024,512]{1,0:T(8,128)(2,1)S(1)}, bf16[1024,512]{1,0:T(8,128)(2,1)S(1)}, u32[]{:S(2)}, u32[]{:S(2)}) %collective-permute-start.4) | collective-permute-done | bytes 1048608 | tf_op jit(solution)/shard_map/ppermute | solution.py:22
  105.2 0.0 copy-start.5
  105.2 1.0 copy-done.5
  106.1 0.0 collective-permute-start.5
  106.1 16.1 %collective-permute-done.5 = bf16[1024,512]{1,0:T(8,128)(2,1)} collective-permute-done((bf16[1024,512]{1,0:T(8,128)(2,1)S(1)}, bf16[1024,512]{1,0:T(8,128)(2,1)}, u32[]{:S(2)}, u32[]{:S(2)}) %collective-permute-start.5) | collective-permute-done | bytes 1048608 | tf_op jit(solution)/shard_map/ppermute | solution.py:22
  122.2 0.0 collective-permute-start.6
  122.3 0.0 copy-start.6
  122.3 0.0 copy-start.4
  122.3 0.0 copy-start.2
  122.3 0.8 convert_convert_fusion
  123.1 15.5 %collective-permute-done.6 = bf16[1024,512]{1,0:T(8,128)(2,1)} collective-permute-done((bf16[1024,512]{1,0:T(8,128)(2,1)}, bf16[1024,512]{1,0:T(8,128)(2,1)}, u32[]{:S(2)}, u32[]{:S(2)}) %collective-permute-start.6) | collective-permute-done | bytes 1048608 | tf_op jit(solution)/shard_map/ppermute | solution.py:22
  138.6 2.6 constant_dynamic-update-slice_fusion.15
  141.2 2.3 constant_dynamic-update-slice_fusion.14
  143.4 2.3 constant_dynamic-update-slice_fusion.13
  145.7 2.3 constant_dynamic-update-slice_fusion.12
  147.9 2.3 constant_dynamic-update-slice_fusion.11
  150.2 1.0 constant_dynamic-update-slice_fusion.10
  151.2 1.0 constant_dynamic-update-slice_fusion.9
  152.3 0.0 copy-done
  152.3 1.3 constant_dynamic-update-slice_fusion.8
  153.5 2.3 constant_dynamic-update-slice_fusion.7
  155.8 2.3 constant_dynamic-update-slice_fusion.6
  158.1 0.0 copy-done.6
  158.1 1.0 constant_dynamic-update-slice_fusion.5
  159.1 0.0 copy-done.4
  159.1 1.0 constant_dynamic-update-slice_fusion.4
  160.1 0.0 copy-done.2
  160.2 1.0 constant_dynamic-update-slice_fusion.3
  161.2 1.0 constant_dynamic-update-slice_fusion.2
  162.2 1.0 constant_dynamic-update-slice_fusion.1
  163.3 1.3 constant_dynamic-update-slice_fusion
  164.5 7.7 %constant_dynamic-slice_fusion = bf16[1024,4096]{1,0:T(8,128)(2,1)} fusion(bf16[1024,8192]{1,0:T(8,128)(2,1)} %constant_dynamic-update-slice_fusion, s32[]{:T(128)S(6)} %select_n.14), kind=kLoop, calls=%fused_computation.48 | loop fusion | bytes 16777220 | tf_op jit(solution)/shard_map/jit(_roll_dynamic)/dynamic_slice | solution.py:23
  172.2 140.9 %all-gather.2.cloned.1.call-done = bf16[3,1376,4096]{2,1,0:T(8,128)(2,1)} async-done(((bf16[3,1376,1024]{2,1,0:T(8,128)(2,1)}), bf16[3,1376,4096]{2,1,0:T(8,128)(2,1)}) %all-gather.2.cloned.1.call-update) | async-done | bytes 33816592 | tf_op jit(solution)/shard_map/all_gather | solution.py:38
  313.1 45.7 %fusion.19 = (bf16[1024,1376]{0,1:T(8,128)(2,1)}, bf16[1024,1376]{0,1:T(8,128)(2,1)}, bf16[1024,1376]{0,1:T(8,128)(2,1)}) fusion(bf16[1024,1376]{0,1:T(8,128)(2,1)} %param.7, bf16[1024,1376]{0,1:T(8,128)(2,1)} %param.8, bf16[3,1376,4096]{2,1,0:T(8,128)(2,1)} %all-gather.2.cloned.1.call-done, bf16[3,1024]{1,0:T(4,128)(2,1)S(1)} %convert_convert_fusion, ...), kind=kOutput, calls=%fused_computation.23 | convolution fusion | flops 34664710144 | bytes 56301568 | tf_op jit(solution)/shard_map/dot_general | solution.py:36
  358.8 2.9 fusion.28
  361.7 41.2 %fusion.4 = bf16[3,1376,4096]{2,1,0:T(8,128)(2,1)} fusion(bf16[3,1024]{1,0:T(4,128)(2,1)S(1)} %convert_convert_fusion, bf16[1024,4096]{1,0:T(8,128)(2,1)} %constant_dynamic-slice_fusion, bf16[3,1024,1376]{1,2,0:T(8,128)(2,1)S(1)} %fusion.28), kind=kOutput, calls=%fused_computation.4 | convolution fusion | flops 34657665024 | bytes 50665472 | tf_op jit(solution)/shard_map/dot_general | solution.py:46
  402.9 0.0 reduce-scatter.2.cloned.1.call-update
  402.9 290.8 %reduce-scatter.2.cloned.1.call-done = bf16[3,1376,1024]{2,1,0:T(8,128)(2,1)} async-done(((bf16[3,1376,4096]{2,1,0:T(8,128)(2,1)}), bf16[3,1376,1024]{2,1,0:T(8,128)(2,1)}) %reduce-scatter.2.cloned.1.call-update) | async-done | bytes 8454160 | tf_op jit(solution)/shard_map/reduce_scatter | solution.py:49
  693.8 11.8 %convert_element_type.53 = f32[3,1376,1024]{2,1,0:T(8,128)} convert(bf16[3,1376,1024]{2,1,0:T(8,128)(2,1)} %reduce-scatter.2.cloned.1.call-done) | non-fusion elementwise | flops 4227072 | bytes 25362432 | tf_op jit(solution)/shard_map/convert_element_type | solution.py:51
  (1 shorter events, 0.0 us)
Async XLA Ops:
  7.2 145.1 %copy-start = (bf16[1024,512]{1,0:T(8,128)(2,1)S(1)}, bf16[1024,512]{1,0:T(8,128)(2,1)}, u32[]{:S(2)}) copy-start(bf16[1024,512]{1,0:T(8,128)(2,1)} %param.6) | copy-start | bytes 3145732
  7.2 305.9 %all-gather.2.cloned.1.call-start = ((), (), s32[]{:S(2)}) async-start(), calls=%async_computation.2 | async-start | bytes 42270720 | tf_op jit(solution)/shard_map/all_gather | solution.py:38
  7.9 685.9 %reduce-scatter.2.cloned.1.call-start = ((), (), s32[]{:S(2)}) async-start(), calls=%async_computation.1 | async-start | bytes 42270720 | tf_op jit(solution)/shard_map/reduce_scatter | solution.py:49
  23.0 16.1 %collective-permute-start = (bf16[1024,512]{1,0:T(8,128)(2,1)S(1)}, bf16[1024,512]{1,0:T(8,128)(2,1)S(1)}, u32[]{:S(2)}, u32[]{:S(2)}) collective-permute-start(bf16[1024,512]{1,0:T(8,128)(2,1)S(1)} %multiply_convert_fusion), channel_id=1, source_target_pairs={{0,1},{1,2},{2,3},{3,4},{4,5},{5,6},{6,7},{7,0},{8,9},{9,10},{10,1... | collective-permute-start | bytes 3145736 | tf_op jit(solution)/shard_map/ppermute | solution.py:22
  39.1 16.0 %collective-permute-start.1 = (bf16[1024,512]{1,0:T(8,128)(2,1)S(1)}, bf16[1024,512]{1,0:T(8,128)(2,1)S(1)}, u32[]{:S(2)}, u32[]{:S(2)}) collective-permute-start(bf16[1024,512]{1,0:T(8,128)(2,1)S(1)} %collective-permute-done), channel_id=1, source_target_pairs={{0,1},{1,2},{2,3},{3,4},{4,5},{5,6},{6,7},{7,0},{8,9},{9,10},{10,1... | collective-permute-start | bytes 3145736 | tf_op jit(solution)/shard_map/ppermute | solution.py:22
  55.1 16.0 %collective-permute-start.2 = (bf16[1024,512]{1,0:T(8,128)(2,1)S(1)}, bf16[1024,512]{1,0:T(8,128)(2,1)S(1)}, u32[]{:S(2)}, u32[]{:S(2)}) collective-permute-start(bf16[1024,512]{1,0:T(8,128)(2,1)S(1)} %collective-permute-done.1), channel_id=1, source_target_pairs={{0,1},{1,2},{2,3},{3,4},{4,5},{5,6},{6,7},{7,0},{8,9},{9,10},{10,1... | collective-permute-start | bytes 3145736 | tf_op jit(solution)/shard_map/ppermute | solution.py:22
  71.1 1.0 copy-start.1
  72.1 16.0 %collective-permute-start.3 = (bf16[1024,512]{1,0:T(8,128)(2,1)S(1)}, bf16[1024,512]{1,0:T(8,128)(2,1)S(1)}, u32[]{:S(2)}, u32[]{:S(2)}) collective-permute-start(bf16[1024,512]{1,0:T(8,128)(2,1)S(1)} %collective-permute-done.2), channel_id=1, source_target_pairs={{0,1},{1,2},{2,3},{3,4},{4,5},{5,6},{6,7},{7,0},{8,9},{9,10},{10,1... | collective-permute-start | bytes 3145736 | tf_op jit(solution)/shard_map/ppermute | solution.py:22
  88.2 1.0 copy-start.3
  89.1 16.0 %collective-permute-start.4 = (bf16[1024,512]{1,0:T(8,128)(2,1)S(1)}, bf16[1024,512]{1,0:T(8,128)(2,1)S(1)}, u32[]{:S(2)}, u32[]{:S(2)}) collective-permute-start(bf16[1024,512]{1,0:T(8,128)(2,1)S(1)} %collective-permute-done.3), channel_id=1, source_target_pairs={{0,1},{1,2},{2,3},{3,4},{4,5},{5,6},{6,7},{7,0},{8,9},{9,10},{10,1... | collective-permute-start | bytes 3145736 | tf_op jit(solution)/shard_map/ppermute | solution.py:22
  105.2 1.0 copy-start.5
  106.1 16.1 %collective-permute-start.5 = (bf16[1024,512]{1,0:T(8,128)(2,1)S(1)}, bf16[1024,512]{1,0:T(8,128)(2,1)}, u32[]{:S(2)}, u32[]{:S(2)}) collective-permute-start(bf16[1024,512]{1,0:T(8,128)(2,1)S(1)} %collective-permute-done.4), channel_id=1, source_target_pairs={{0,1},{1,2},{2,3},{3,4},{4,5},{5,6},{6,7},{7,0},{8,9},{9,10},{10,1... | collective-permute-start | bytes 3145736 | tf_op jit(solution)/shard_map/ppermute | solution.py:22
  122.2 16.3 %collective-permute-start.6 = (bf16[1024,512]{1,0:T(8,128)(2,1)}, bf16[1024,512]{1,0:T(8,128)(2,1)}, u32[]{:S(2)}, u32[]{:S(2)}) collective-permute-start(bf16[1024,512]{1,0:T(8,128)(2,1)} %collective-permute-done.5), channel_id=1, source_target_pairs={{0,1},{1,2},{2,3},{3,4},{4,5},{5,6},{6,7},{7,0},{8,9},{9,10},{10,1... | collective-permute-start | bytes 3145736 | tf_op jit(solution)/shard_map/ppermute | solution.py:22
  122.3 35.8 %copy-start.6 = (bf16[1024,512]{1,0:T(8,128)(2,1)S(1)}, bf16[1024,512]{1,0:T(8,128)(2,1)}, u32[]{:S(2)}) copy-start(bf16[1024,512]{1,0:T(8,128)(2,1)} %copy-done.5) | copy-start | bytes 3145732
  122.3 36.9 %copy-start.4 = (bf16[1024,512]{1,0:T(8,128)(2,1)S(1)}, bf16[1024,512]{1,0:T(8,128)(2,1)}, u32[]{:S(2)}) copy-start(bf16[1024,512]{1,0:T(8,128)(2,1)} %copy-done.3) | copy-start | bytes 3145732
  122.3 37.9 %copy-start.2 = (bf16[1024,512]{1,0:T(8,128)(2,1)S(1)}, bf16[1024,512]{1,0:T(8,128)(2,1)}, u32[]{:S(2)}) copy-start(bf16[1024,512]{1,0:T(8,128)(2,1)} %copy-done.1) | copy-start | bytes 3145732
Sparse Core Ops, SparseCore 0:
  9.9 303.2 all-gather.1
  403.0 290.6 reduce-scatter.1
